TPU v7x, 128 devices: a whole 4x4x4 slice. The times are simulated.
128 devices in a mesh: dp: 32 (over z, y, core), mp: 4 (over x).
Axes of the slice: x: 4, y: 4, z: 4, core: 2. Of those that a mesh axis runs over, the one named last changes fastest.
Arguments:
- ids: int32 [32768], P('dp'), may hold values from 0 to 16777215, as said below
- hash_a: int32 [1024], replicated, may hold values from 1 to 16383
- hash_b: int32 [1024], replicated, may hold values from 0 to 16383
- hash_p: int32 [1024], replicated, may hold values from 16384 to 32767
- hash_m: int32 [1024], replicated, may hold values from 4096 to 16383
- w_in: bfloat16 [1024, 2048], P(None, 'mp'), may hold values from -0.1875 to 0.1875
- w_mid: bfloat16 [2, 2048, 2048], P(None, None, 'mp'), may hold values from -0.125 to 0.125
- w_out: bfloat16 [2048, 64], P('mp'), may hold values from -0.125 to 0.125
- bn_gain: float32 [3, 2048], P(None, 'mp'), may hold values from 0.25 to 1.75
- bn_bias: float32 [3, 2048], P(None, 'mp'), may hold values from -3 to 3
- target: float32 [32768, 64], P('dp'), may hold values from -6 to 6
Outputs:
- grad_w_in: float32 [1024, 2048], P('dp', 'mp')
- grad_w_mid: float32 [2, 2048, 2048], P(None, 'dp', 'mp')
- grad_w_out: float32 [2048, 64], P(('mp', 'dp'))
- grad_gain: float32 [3, 2048], P(None, 'mp')
- grad_bias: float32 [3, 2048], P(None, 'mp')
Inputs may be any that keep to these rules, and one draw needn't show every extreme that they name: The number of distinct ids among one device's 1024 rows differs from device to device, from one to many.
All inputs are finite; a program needn't handle non-finite values.
Results may differ from a plain program's by a relative error of at most 0.02.
Values may be sent and summed in bfloat16 or wider, within the bound.
No kernel may reach another device: no remote copies, remote signals or barrier semaphores. Data moves between devices by JAX's collectives and lax.ppermute only.
A program may use at most 128 MiB of HBM per device.

v0:
```python
import math

import jax
import jax.numpy as jnp
from jax import lax
from jax.experimental import pallas as pl
from jax.sharding import Mesh, PartitionSpec as P

epsilon_norm = 1e-05
plane = ("z", "y")
over_chips = (("z", "y", "x"),)
over_chips_x_last = (("z", "y"), "x")
over_rows = ("c", ("z", "y"))
rows_axes = ("z", "y", "c")
float32 = jnp.float32
bfloat16 = jnp.bfloat16


def swap_cores(array):
    return lax.ppermute(array, "c", [(0, 1), (1, 0)])


def from_everyone(array, axis):
    size = lax.axis_size(axis)
    return lax.all_to_all(
        jnp.broadcast_to(array[None], (size, *array.shape)), axis, 0, 0, tiled=True
    )


def sum_over(rows, stages):
    for axis in stages:
        if axis == "c":
            rows = rows + swap_cores(rows)
        else:
            rows = jnp.sum(from_everyone(rows, axis), axis=0)
    return rows[0]


def total_of(pair, stages):
    return jnp.split(sum_over(jnp.concatenate(pair)[None], stages), len(pair))


def float_mod(values, inverse, modulus):
    rest = values - jnp.floor(values * inverse) * modulus
    return jnp.where(rest >= modulus, rest - modulus, rest)


def encode(ids, hash_a, hash_b, hash_p, hash_m):
    modulus = hash_p.astype(float32)[None, :]
    buckets = hash_m.astype(float32)[None, :]
    below = 1.0 - 2.0**-21
    inverse_p = below / modulus
    inverse_m = below / buckets
    high = (hash_a // 128).astype(float32)[None, :]
    low = (hash_a % 128).astype(float32)[None, :]
    shift = hash_b.astype(float32)[None, :]
    step = 2.0 / (buckets - 1.0)
    reduced = float_mod(ids.astype(float32)[:, None], inverse_p, modulus)
    carried = float_mod(high * reduced, inverse_p, modulus)
    mixed = float_mod(carried * 128.0 + low * reduced + shift, inverse_p, modulus)
    hashed = float_mod(mixed, inverse_m, buckets)
    return lax.optimization_barrier((hashed * step - 1.0).astype(bfloat16))


def mish_act(values):
    power = jnp.exp(jnp.minimum(values, 30.0))
    ratio = power * (power + 2.0)
    return values * (ratio / (ratio + 2.0))


def mish_slope(values):
    power = jnp.exp(jnp.minimum(values, 30.0))
    ratio = power * (power + 2.0)
    inverse = 1.0 / (ratio + 2.0)
    return inverse * (ratio + 4.0 * values * (power * (power + 1.0)) * inverse)


def dot(left, right):
    return jnp.dot(left, right, preferred_element_type=float32)


def dot_rows(left, right):
    return lax.dot_general(left, right, (((0,), (0,)), ((), ())), preferred_element_type=float32)


def dot_back(left, right):
    return lax.dot_general(left, right, (((1,), (1,)), ((), ())), preferred_element_type=float32)


def layer_dot(inputs, weights):
    part, units = inputs[0].shape
    rows, width = part * len(inputs), weights[0].shape[1]
    block = min(256, width)

    def body(*refs):
        input_refs, weight_refs = refs[: len(inputs)], refs[len(inputs) : -2]
        totals, squares = 0.0, 0.0
        for at, input_ref in enumerate(input_refs):
            product = 0.0
            start = 0
            for ref in weight_refs:
                end = start + ref.shape[0]
                product = product + dot(input_ref[:, start:end], ref[...])
                start = end
            refs[-2][at * part : (at + 1) * part, :] = product
            totals = totals + jnp.sum(product, axis=0, keepdims=True)
            squares = squares + jnp.sum(product * product, axis=0, keepdims=True)
        refs[-1][0:1, :] = totals
        refs[-1][1:2, :] = squares

    return pl.pallas_call(
        body,
        grid=(width // block,),
        in_specs=[pl.BlockSpec((part, units), lambda n: (0, 0)) for _ in inputs]
        + [pl.BlockSpec((w.shape[0], block), lambda n: (0, n)) for w in weights],
        out_specs=[
            pl.BlockSpec((rows, block), lambda n: (0, n)),
            pl.BlockSpec((2, block), lambda n: (0, n)),
        ],
        out_shape=[
            jax.ShapeDtypeStruct((rows, width), float32),
            jax.ShapeDtypeStruct((2, width), float32),
        ],
        cost_estimate=pl.CostEstimate(
            flops=2 * rows * units * width,
            transcendentals=0,
            bytes_accessed=2 * rows * units + 2 * units * width + 4 * rows * width,
        ),
    )(*inputs, *weights)


def back_dot(slopes, weights, half):
    rows, width = slopes.shape
    middle = rows // 2

    def body(slope_ref, weight_ref, keep_ref, send_ref):
        product = dot_back(slope_ref[...], weight_ref[...])
        keep_ref[...] = product[:, :half]
        send_ref[:middle, :] = product[middle:, half:].astype(bfloat16)
        send_ref[middle:, :] = product[:middle, half:].astype(bfloat16)

    units = weights.shape[0] // 2
    return pl.pallas_call(
        body,
        grid=(units // half,),
        in_specs=[
            pl.BlockSpec(slopes.shape, lambda n: (0, 0)),
            pl.BlockSpec((2 * half, width), lambda n: (n, 0)),
        ],
        out_specs=[
            pl.BlockSpec((rows, half), lambda n: (0, n)),
            pl.BlockSpec((rows, half), lambda n: (0, n)),
        ],
        out_shape=[
            jax.ShapeDtypeStruct((rows, units), float32),
            jax.ShapeDtypeStruct((rows, units), bfloat16),
        ],
        cost_estimate=pl.CostEstimate(
            flops=4 * rows * width * units,
            transcendentals=0,
            bytes_accessed=2 * slopes.size + 2 * weights.size + 6 * rows * units,
        ),
    )(slopes, weights)


def weight_dot(inputs, slopes):
    part, units = inputs[0].shape
    width = slopes.shape[1]
    block = min(512, units)

    def body(*refs):
        slope_ref, out_ref = refs[-2:]
        product = 0.0
        for at, ref in enumerate(refs[:-2]):
            product = product + dot_rows(ref[...], slope_ref[at * part : (at + 1) * part, :])
        out_ref[...] = product.astype(bfloat16)

    return pl.pallas_call(
        body,
        grid=(units // block,),
        in_specs=[pl.BlockSpec((part, block), lambda n: (0, n)) for _ in inputs]
        + [pl.BlockSpec(slopes.shape, lambda n: (0, 0))],
        out_specs=pl.BlockSpec((block, width), lambda n: (n, 0)),
        out_shape=jax.ShapeDtypeStruct((units, width), bfloat16),
        cost_estimate=pl.CostEstimate(
            flops=2 * slopes.size * units,
            transcendentals=0,
            bytes_accessed=2 * slopes.shape[0] * units + 2 * slopes.size + 2 * units * width,
        ),
    )(*inputs, slopes)


def split_back_dot(slopes, top, end):
    rows, width = slopes.shape
    middle = rows // 2
    units = top.shape[0]
    block = min(512, units)
    steps = units // block

    def body(slope_ref, top_ref, end_ref, keep_ref, send_ref):
        def write(weight_ref):
            product = dot_back(slope_ref[...], weight_ref[...])
            keep_ref[...] = product[:middle]
            send_ref[...] = product[middle:].astype(bfloat16)

        at = pl.program_id(0)
        pl.when(at < steps)(lambda: write(top_ref))
        pl.when(at >= steps)(lambda: write(end_ref))

    return pl.pallas_call(
        body,
        grid=(2 * steps,),
        in_specs=[
            pl.BlockSpec(slopes.shape, lambda n: (0, 0)),
            pl.BlockSpec((block, width), lambda n: (jnp.minimum(n, steps - 1), 0)),
            pl.BlockSpec((block, width), lambda n: (jnp.maximum(n - steps, 0), 0)),
        ],
        out_specs=[
            pl.BlockSpec((middle, block), lambda n: (0, n)),
            pl.BlockSpec((middle, block), lambda n: (0, n)),
        ],
        out_shape=[
            jax.ShapeDtypeStruct((middle, 2 * units), float32),
            jax.ShapeDtypeStruct((middle, 2 * units), bfloat16),
        ],
        cost_estimate=pl.CostEstimate(
            flops=4 * rows * width * units,
            transcendentals=0,
            bytes_accessed=2 * slopes.size + 4 * units * width + 12 * middle * units,
        ),
    )(slopes, top, end)


def normalise(sums, axis, batch_total):
    totals, squares = total_of(sums, axis)
    average = totals / batch_total
    spread = squares / batch_total - average * average
    return average, 1.0 / jnp.sqrt(spread + epsilon_norm)


def flip_rows(array):
    half = array.shape[0] // 2
    return jnp.concatenate([array[half:], array[:half]])


def step(ids, hash_a, hash_b, hash_p, hash_m, w_in, w_mid, w_out, bn_gain, bn_bias, target):
    core = lax.axis_index("c")
    lane = lax.axis_index("x")
    first = core == 0
    mp = lax.axis_size("x")
    depth, height = lax.axis_size("z"), lax.axis_size("y")
    planes = depth * height
    rows, batch_devices = ids.shape[0], lax.axis_size(rows_axes)
    batch_total = rows * batch_devices
    width = w_in.shape[1]
    half = width // 2
    own = mp * half
    hidden = mp * width
    part = rows // mp
    out = w_out.shape[1]

    def in_order(mine, other):
        return jnp.where(first, mine, other), jnp.where(first, other, mine)

    def weight_part(layer, row, count):
        start = (layer, row, core * half)
        return lax.dynamic_slice(w_mid, start, (1, count, half)).reshape(count, half)

    w2_top = lax.all_gather(weight_part(0, 0, own), "x", axis=1, tiled=True)
    w2_near = weight_part(0, own, own)
    w2_far = [w2_near] + [
        lax.ppermute(w2_near, "x", [(i, i ^ k) for i in range(mp)]) for k in range(1, mp)
    ]
    w2_end = jnp.concatenate([lax.select_n(lane ^ k, *w2_far) for k in range(mp)], axis=1)
    w3_low, w3_high = jnp.split(weight_part(1, 0, hidden).reshape(mp, 2, half, half), 2, axis=1)
    w3_part = jnp.concatenate(in_order(w3_low, w3_high), axis=1).reshape(hidden, half)
    w3 = lax.all_gather(w3_part, "x", axis=1, tiled=True)

    def half_of(array, axis):
        return lax.dynamic_slice_in_dim(array, core * half, half, axis=axis)

    vectors = jnp.concatenate([half_of(bn_gain[1:], 1), half_of(bn_bias[1:], 1)])
    high = lax.reduce_precision(vectors, 8, 7)
    middle = lax.reduce_precision(vectors - high, 8, 7)
    low = vectors - high - middle
    small = jnp.concatenate(
        [
            half_of(w_out, 0).reshape(-1, width),
            jnp.concatenate([high, middle, low]).astype(bfloat16).reshape(-1, width),
        ]
    )
    small = jnp.pad(small, ((0, -small.shape[0] % 16), (0, 0)))
    target_own = lax.dynamic_slice_in_dim(target, lane * part, part, axis=0)
    wanted = jnp.concatenate([target_own, swap_cores(target_own)])

    encoded = encode(ids, hash_a, hash_b, hash_p, hash_m)
    z1 = dot(encoded, w_in)
    sums1 = (jnp.sum(z1, axis=0), jnp.sum(z1 * z1, axis=0))
    mean1, inv1 = normalise(sums1, over_rows, batch_total)
    n1 = (z1 - mean1) * inv1
    a1 = bn_gain[0] * n1 + bn_bias[0]
    x1 = mish_act(a1).astype(bfloat16)
    message = jnp.concatenate(
        [x1.reshape(mp, part, width), jnp.broadcast_to(small[None], (mp, *small.shape))], axis=1
    )
    message = lax.all_to_all(message, "x", 0, 0, tiled=True)
    x1_own = jnp.concatenate(list(message[:, :part]), axis=1)
    x1_other = swap_cores(x1_own)
    small = message[:, part:].reshape(mp, -1)
    w_out_own = small[:, : half * out].reshape(own, out)
    vectors = small[:, half * out : half * out + 12 * half].astype(float32)
    vectors = vectors.reshape(mp, 3, 4, half)
    vectors = vectors[:, 0] + vectors[:, 1] + vectors[:, 2]
    gain2, gain3, bias2, bias3 = vectors.transpose(1, 0, 2).reshape(4, own)
    z2, sums2 = layer_dot((x1_own, x1_other), (w2_top, w2_end))
    mean2, inv2 = normalise((sums2[0], sums2[1]), over_chips_x_last, batch_total)
    n2 = (z2 - mean2) * inv2
    a2 = gain2 * n2 + bias2
    x2 = mish_act(a2).astype(bfloat16)
    x2_other = swap_cores(flip_rows(x2))
    blocks = zip(jnp.split(x2, mp, axis=1), jnp.split(x2_other, mp, axis=1))
    x2_all = jnp.concatenate([block for pair in blocks for block in pair], axis=1)
    z3, sums3 = layer_dot((x2_all,), (w3,))
    mean3, inv3 = normalise((sums3[0], sums3[1]), over_chips, batch_total)
    n3 = (z3 - mean3) * inv3
    a3 = gain3 * n3 + bias3
    x3 = mish_act(a3).astype(bfloat16)

    y_part = dot(x3, w_out_own)
    predicted = y_part + swap_cores(flip_rows(y_part))
    g_y = ((predicted - wanted) / math.sqrt(batch_total)).astype(bfloat16)
    g_out = dot_rows(x3, g_y).reshape(mp, planes // 2, 2, -1, out)
    keep_out = jnp.where(first, g_out[:, :, 0], g_out[:, :, 1])
    send_out = jnp.where(first, g_out[:, :, 1], g_out[:, :, 0]).astype(bfloat16)
    keep_out = keep_out.astype(bfloat16)
    g_out = jnp.stack(in_order(keep_out, swap_cores(send_out)))
    g_out = g_out.transpose(0, 2, 1, 3, 4).reshape(depth, height * mp, -1)
    g_out = g_out.transpose(1, 0, 2).reshape(height * mp, 1, -1).astype(float32)

    u3 = dot_back(g_y, w_out_own)
    s3 = u3 * mish_slope(a3)
    bias_sum3, gain_sum3 = total_of((jnp.sum(s3, axis=0), jnp.sum(s3 * n3, axis=0)), over_chips)
    e3 = (gain3 * inv3 * (s3 - bias_sum3 / batch_total - n3 * gain_sum3 / batch_total)).astype(
        bfloat16
    )
    u2_keep, u2_send = back_dot(e3, w3, half)
    u2 = u2_keep + swap_cores(u2_send).astype(float32)
    dw3 = weight_dot((x2_all,), e3)
    dw3 = lax.psum_scatter(dw3, "z", scatter_dimension=0, tiled=True)
    dw3 = lax.psum_scatter(dw3, "x", scatter_dimension=1, tiled=True)

    s2 = u2 * mish_slope(a2)
    sums2 = jnp.concatenate([jnp.sum(s2, axis=0), jnp.sum(s2 * n2, axis=0)])
    count = sums2.shape[0]
    sums2 = jnp.broadcast_to(sums2[None, None], (height * mp, 1, count))
    sums2 = jnp.concatenate([sums2, g_out], axis=2)
    sums2 = jnp.sum(lax.all_to_all(sums2, ("y", "x"), 0, 0, tiled=True), axis=(0, 1))
    g_out = sums2[count:].reshape(depth, -1)
    sums2 = jnp.broadcast_to(sums2[None, :count], (depth, count))
    sums2 = jnp.concatenate([sums2, g_out], axis=1)[:, None]
    sums2 = jnp.sum(lax.all_to_all(sums2, "z", 0, 0, tiled=True), axis=(0, 1))
    bias_sum2, gain_sum2 = sums2[:own], sums2[own:count]
    grad_out = sums2[count:].reshape(-1, out)
    e2 = (gain2 * inv2 * (s2 - bias_sum2 / batch_total - n2 * gain_sum2 / batch_total)).astype(
        bfloat16
    )
    u1_keep, u1_send = split_back_dot(e2, w2_top, w2_end)
    u1_own = (u1_keep + swap_cores(u1_send).astype(float32)).astype(bfloat16)
    u1 = lax.all_to_all(u1_own, "x", 1, 0, tiled=True).astype(float32)
    dw2 = weight_dot((x1_own, x1_other), e2)
    dw2 = lax.psum_scatter(dw2, "z", scatter_dimension=0, tiled=True)
    dw2 = jnp.stack([b.reshape(height, -1, half) for b in jnp.split(dw2, mp, axis=1)], axis=1)
    dw2 = lax.all_to_all(dw2.reshape(height * mp, -1, half), ("y", "x"), 0, 0, tiled=True)
    dw2 = jnp.sum(dw2.astype(float32), axis=0)

    s1 = u1 * mish_slope(a1)
    bias_sum1, gain_sum1 = total_of((jnp.sum(s1, axis=0), jnp.sum(s1 * n1, axis=0)), over_rows)
    e1 = (
        bn_gain[0] * inv1 * (s1 - bias_sum1 / batch_total - n1 * gain_sum1 / batch_total)
    ).astype(bfloat16)
    dw1 = dot_rows(encoded, e1).reshape(planes, 2, -1, width)
    keep1 = jnp.where(first, dw1[:, 0], dw1[:, 1])
    send1 = jnp.where(first, dw1[:, 1], dw1[:, 0]).astype(bfloat16)
    dw1 = (keep1 + swap_cores(send1).astype(float32)).astype(bfloat16)
    dw1 = lax.all_to_all(dw1, plane, 0, 0, tiled=True)
    grad_first = jnp.sum(dw1.astype(float32), axis=0)

    dw2, dw3, grad_first = lax.optimization_barrier((dw2, dw3, grad_first))
    dw3 = dw3.reshape(2, half, half)
    dw3 = jnp.stack(in_order(dw3[0], dw3[1])).reshape(height, -1, half)
    dw3 = jnp.sum(lax.all_to_all(dw3, "y", 0, 0, tiled=True).astype(float32), axis=0)
    last = jnp.stack([dw2, dw3])
    low, high = jnp.split(last, 2, axis=1)
    other = swap_cores(jnp.where(first, high, low))
    grad_mid = jnp.concatenate(in_order(jnp.where(first, low, high), other), axis=2)

    sums = jnp.stack([gain_sum2, gain_sum3, bias_sum2, bias_sum3]).reshape(4, mp, half)
    mine = lax.dynamic_index_in_dim(sums, lane, axis=1, keepdims=False)
    later = jnp.concatenate(in_order(mine, swap_cores(mine)), axis=1)
    grad_gain = jnp.stack([gain_sum1, later[0], later[1]])
    grad_bias = jnp.stack([bias_sum1, later[2], later[3]])
    return (grad_first, grad_mid, grad_out, grad_gain, grad_bias)


def solution(mesh):
    grid = Mesh(mesh.devices.reshape(4, 4, 2, 4), ("z", "y", "c", "x"))
    return jax.shard_map(
        step,
        mesh=grid,
        in_specs=(
            P(rows_axes),
            P(),
            P(),
            P(),
            P(),
            P(None, "x"),
            P(None, None, "x"),
            P("x", None),
            P(None, "x"),
            P(None, "x"),
            P(rows_axes, None),
        ),
        out_specs=(
            P(rows_axes, "x"),
            P(None, rows_axes, "x"),
            P(("x", "z", "y", "c"), None),
            P(None, "x"),
            P(None, "x"),
        ),
        check_vma=False,
    )
```

profile of v0, /device:TPU:1, one launch (start us, length us, event | category | flops | bytes accessed | tf_op | source)
XLA Modules:
  0.0 351.0 jit_solution(929249956334988286)
XLA Ops:
  7.3 2.3 dynamic-slice_bitcast_fusion
  9.6 3.3 collective-permute-start.4
  13.6 5.2 %fusion.5 = bf16[1024,1024]{1,0:T(8,128)(2,1)S(1)} fusion(f32[1024]{0:T(1024)S(1)} %get-tuple-element.96, f32[1024]{0:T(1024)S(1)} %convert_element_type.129, f32[1024]{0:T(1024)S(1)} %get-tuple-element.95, f32[1024]{0:T(1024)S(1)} %convert_element_type.128, f32[1024]{0:T(1024)S(1)} %get-tuple-element.94, f32[1024]{0:T(1024)S(1)} %convert_element_type.126, ...), kind=kLoop, calls=%fused_computation.9 | loop fusion | flops 37748736 | bytes 2134016 | tf_op jit(solution)/shard_map/convert_element_type | solution.py:62
  23.4 7.9 %all-to-all-start = ((f32[16,1,1024]{2,1,0:T(1,128)}), f32[16,1,1024]{2,1,0:T(1,128)S(1)}, u32[]{:S(2)}, u32[]{:S(2)}) async-start(f32[16,1,1024]{2,1,0:T(1,128)} %broadcast_in_dim.30), calls=%async_computation | async-start | bytes 131072 | tf_op jit(solution)/shard_map/all_to_all | solution.py:25
  31.3 6.5 %all-to-all-done = f32[16,1,1024]{2,1,0:T(1,128)S(1)} async-done(((f32[16,1,1024]{2,1,0:T(1,128)}), f32[16,1,1024]{2,1,0:T(1,128)S(1)}, u32[]{:S(2)}, u32[]{:S(2)}) %all-to-all-start) | async-done | bytes 65568 | tf_op jit(solution)/shard_map/all_to_all | solution.py:25
  40.0 4.0 %all-to-all-start.1 = ((bf16[4,304,512]{2,1,0:T(8,128)(2,1)}), bf16[4,304,512]{2,1,0:T(8,128)(2,1)S(1)}, u32[]{:S(2)}, u32[]{:S(2)}) async-start(bf16[4,304,512]{2,1,0:T(8,128)(2,1)} %pad_maximum_fusion.1), calls=%async_computation.1 | async-start | bytes 2490368 | tf_op jit(solution)/shard_map/all_to_all | solution.py:306
  48.4 20.8 %all-to-all-done.1 = bf16[4,304,512]{2,1,0:T(8,128)(2,1)S(1)} async-done(((bf16[4,304,512]{2,1,0:T(8,128)(2,1)}), bf16[4,304,512]{2,1,0:T(8,128)(2,1)S(1)}, u32[]{:S(2)}, u32[]{:S(2)}) %all-to-all-start.1) | async-done | bytes 1245216 | tf_op jit(solution)/shard_map/all_to_all | solution.py:306
  74.2 6.4 %shard_map.146 = (f32[512,1024]{1,0:T(8,128)}, f32[2,1024]{1,0:T(2,128)}) custom-call(bf16[256,2048]{1,0:T(8,128)(2,1)} %pad_maximum_fusion.2.refs_0_, bf16[256,2048]{1,0:T(8,128)(2,1)} %collective-permute-done.1.refs_1_, bf16[1024,1024]{1,0:T(8,128)(2,1)} %bitcast.217, bf16[1024,1024]{1,0:T(8,128)(2,1)} %pad_maximum_fusion.refs_3_.end_ref), custom_call_target="tpu_custom_call" | custom-call | flops 2147483648 | bytes 8388608 | tf_op jit(solution)/shard_map/pallas_call | solution.py:111
  82.1 7.8 %all-to-all-start.2 = ((f32[16,1,2048]{2,1,0:T(1,128)}), f32[16,1,2048]{2,1,0:T(1,128)S(1)}, u32[]{:S(2)}, u32[]{:S(2)}) async-start(f32[16,1,2048]{2,1,0:T(1,128)} %broadcast_in_dim.32), calls=%async_computation.2 | async-start | bytes 262144 | tf_op jit(solution)/shard_map/all_to_all | solution.py:25
  90.0 6.8 %all-to-all-done.2 = f32[16,1,2048]{2,1,0:T(1,128)S(1)} async-done(((f32[16,1,2048]{2,1,0:T(1,128)}), f32[16,1,2048]{2,1,0:T(1,128)S(1)}, u32[]{:S(2)}, u32[]{:S(2)}) %all-to-all-start.2) | async-done | bytes 131104 | tf_op jit(solution)/shard_map/all_to_all | solution.py:25
  97.5 3.3 all-to-all-start.3
  100.8 4.8 %all-to-all-done.3 = f32[4,1,2048]{2,1,0:T(1,128)S(1)} async-done(((f32[4,1,2048]{2,1,0:T(1,128)}), f32[4,1,2048]{2,1,0:T(1,128)S(1)}, u32[]{:S(2)}, u32[]{:S(2)}) %all-to-all-start.3) | async-done | bytes 32800 | tf_op jit(solution)/shard_map/all_to_all | solution.py:25
  105.7 2.5 fusion.9
  108.3 3.0 collective-permute-start.5
  111.4 2.2 collective-permute-done.5
  113.9 7.7 %all-gather.4.cloned.1.call-done.refs_1_.weight_ref = bf16[2048,1024]{1,0:T(8,128)(2,1)} async-done(((bf16[2048,256]{1,0:T(8,128)(2,1)}), bf16[2048,1024]{1,0:T(8,128)(2,1)}) %all-gather.4.cloned.1.call-update) | async-done | bytes 4194320 | tf_op jit(solution)/shard_map/all_gather | solution.py:277
  121.7 6.5 %shard_map.147 = (f32[512,1024]{1,0:T(8,128)}, f32[2,1024]{1,0:T(2,128)}) custom-call(bf16[512,2048]{1,0:T(8,128)(2,1)} %copy-done.8, bf16[2048,1024]{1,0:T(8,128)(2,1)} %all-gather.4.cloned.1.call-done.refs_1_.weight_ref), custom_call_target="tpu_custom_call" | custom-call | flops 2147483648 | bytes 8388608 | tf_op jit(solution)/shard_map/pallas_call | solution.py:111
  130.1 10.1 %all-to-all-start.4 = ((f32[64,1,2048]{2,1,0:T(1,128)}), f32[64,1,2048]{2,1,0:T(1,128)S(1)}, u32[]{:S(2)}, u32[]{:S(2)}) async-start(f32[64,1,2048]{2,1,0:T(1,128)} %broadcast_in_dim.34), calls=%async_computation.4 | async-start | bytes 1048576 | tf_op jit(solution)/shard_map/all_to_all | solution.py:25
  140.6 10.5 %all-to-all-done.4 = f32[64,1,2048]{2,1,0:T(1,128)S(1)} async-done(((f32[64,1,2048]{2,1,0:T(1,128)}), f32[64,1,2048]{2,1,0:T(1,128)S(1)}, u32[]{:S(2)}, u32[]{:S(2)}) %all-to-all-start.4) | async-done | bytes 524320 | tf_op jit(solution)/shard_map/all_to_all | solution.py:25
  152.9 3.3 collective-permute-start.6
  158.3 3.0 fusion.64
  161.6 17.3 %all_to_all.73 = f32[64,1,2048]{2,1,0:T(1,128)} all-to-all(f32[64,1,2048]{2,1,0:T(1,128)S(1)} %broadcast_in_dim.35), channel_id=1, replica_groups=mesh['z'=4,'y'=4,'c'=2,'x'=4] {'z','y','x'}, dimensions={0} | all-to-all | bytes 1048576 | tf_op jit(solution)/shard_map/all_to_all | solution.py:25
  180.2 3.2 multiply_convert_fusion.2.slope_ref.refs_1_
  183.5 6.0 %shard_map.150 = bf16[2048,1024]{1,0:T(8,128)(2,1)} custom-call(bf16[512,2048]{1,0:T(8,128)(2,1)} %copy-done.8, bf16[512,1024]{1,0:T(8,128)(2,1)} %multiply_convert_fusion.2.slope_ref.refs_1_), custom_call_target="tpu_custom_call" | custom-call | flops 2147483648 | bytes 7340032 | tf_op jit(solution)/shard_map/pallas_call | solution.py:178
  189.6 6.3 %shard_map.148 = (f32[512,1024]{1,0:T(8,128)}, bf16[512,1024]{1,0:T(8,128)(2,1)}) custom-call(bf16[512,1024]{1,0:T(8,128)(2,1)} %multiply_convert_fusion.2.slope_ref.refs_1_, bf16[2048,1024]{1,0:T(8,128)(2,1)} %all-gather.4.cloned.1.call-done.refs_1_.weight_ref), custom_call_target="tpu_custom_call" | custom-call | flops 2147483648 | bytes 8388608 | tf_op jit(solution)/shard_map/pallas_call | solution.py:143
  198.2 2.1 collective-permute-done.9
  201.9 4.9 %fusion.63 = (f32[1024]{0:T(1024)S(1)}, f32[1024]{0:T(1024)S(1)}, f32[512,1024]{1,0:T(8,128)}) fusion(f32[1024]{0:T(1024)S(1)} %bitcast.163, f32[512,1024]{1,0:T(8,128)S(1)} %copy-done.2, f32[1024]{0:T(1024)S(1)} %bitcast.166, f32[1024]{0:T(1024)S(1)} %bitcast.169, f32[1024]{0:T(1024)S(1)} %bitcast.161, f32[512,1024]{1,0:T(8,128)} %get-tuple-element.20, ...), kind=kLoop, calls=%fused_computation.203 | loop fusion | flops 11532288 | bytes 7364608 | tf_op jit(solution)/shard_map/reduce_sum | solution.py:353
  207.2 12.1 %all_to_all.74 = f32[16,1,6144]{2,1,0:T(1,128)S(1)} all-to-all(f32[16,1,6144]{2,1,0:T(1,128)S(1)} %copy.75), channel_id=1, replica_groups=mesh['z'=4,'y'=4,'c'=2,'x'=4] {'y','x'}, dimensions={0} | all-to-all | bytes 786432 | tf_op jit(solution)/shard_map/all_to_all | solution.py:357
  219.7 7.6 %all_to_all.75 = f32[4,1,3072]{2,1,0:T(1,128)S(1)} all-to-all(f32[4,1,3072]{2,1,0:T(1,128)S(1)} %broadcast_in_dim.38), channel_id=1, replica_groups=mesh['z'=4,'y'=4,'c'=2,'x'=4] {'z'}, dimensions={0} | all-to-all | bytes 98304 | tf_op jit(solution)/shard_map/all_to_all | solution.py:361
  227.4 3.1 multiply_convert_fusion.1.refs_2_.slope_ref
  230.5 6.2 %shard_map.149 = bf16[2048,1024]{1,0:T(8,128)(2,1)} custom-call(bf16[256,2048]{1,0:T(8,128)(2,1)} %pad_maximum_fusion.2.refs_0_, bf16[256,2048]{1,0:T(8,128)(2,1)} %collective-permute-done.1.refs_1_, bf16[512,1024]{1,0:T(8,128)(2,1)} %multiply_convert_fusion.1.refs_2_.slope_ref), custom_call_target="tpu_custom_call" | custom-call | flops 2147483648 | bytes 7340032 | tf_op jit(solution)/shard_map/pallas_call | solution.py:178
  236.8 6.6 %shard_map.151 = (f32[256,2048]{1,0:T(8,128)}, bf16[256,2048]{1,0:T(8,128)(2,1)}) custom-call(bf16[512,1024]{1,0:T(8,128)(2,1)} %multiply_convert_fusion.1.refs_2_.slope_ref, bf16[1024,1024]{1,0:T(8,128)(2,1)} %bitcast.218, bf16[1024,1024]{1,0:T(8,128)(2,1)} %pad_maximum_fusion.refs_3_.end_ref), custom_call_target="tpu_custom_call" | custom-call | flops 2147483648 | bytes 8388608 | tf_op jit(solution)/shard_map/pallas_call | solution.py:210
  243.4 2.9 collective-permute-start.10
  246.3 2.5 collective-permute-done.10
  248.8 1.9 add_convert_fusion
  250.8 17.4 %all_to_all.76 = bf16[256,4,512]{2,0,1:T(8,128)(2,1)S(1)} all-to-all(bf16[256,4,512]{2,0,1:T(8,128)(2,1)S(1)} %bitcast.144), channel_id=1, replica_groups=mesh['z'=4,'y'=4,'c'=2,'x'=4] {'x'}, dimensions={1} | all-to-all | bytes 2097152 | tf_op jit(solution)/shard_map/all_to_all | solution.py:369
  268.2 2.9 fusion.62
  273.3 9.2 %all_to_all.77 = f32[16,1,1024]{2,1,0:T(1,128)S(1)} all-to-all(f32[16,1,1024]{2,1,0:T(1,128)S(1)} %broadcast_in_dim.41), channel_id=1, replica_groups=mesh['z'=4,'y'=4,'c'=2,'x'=4] {'z','y'}, dimensions={0} | all-to-all | bytes 131072 | tf_op jit(solution)/shard_map/all_to_all | solution.py:25
  282.5 3.6 %fusion.27 = f32[1024,512]{1,0:T(8,128)S(1)} fusion(bf16[1024,1024]{1,0:T(8,128)(2,1)} %copy-done.7, f32[1024,512]{1,0:T(8,128)} %get-tuple-element.37, f32[1024,512]{1,0:T(8,128)S(1)} %copy-done.4, f32[512]{0:T(512)S(1)} %bitcast.214, f32[512]{0:T(512)S(1)} %bitcast.216, f32[512]{0:T(512)S(1)} %bitcast.215, f32[512]{0:T(512)S(1)} %bitcast.187, ...), kind=kOutput, calls=%fused_computation.63 | convolution fusion | flops 1077936128 | bytes 8398848 | tf_op jit(solution)/shard_map/dot_general | solution.py:83
  287.6 1.8 collective-permute-start.12
  291.0 2.6 fusion.30
  293.6 3.6 %all-to-all-start.11 = ((bf16[16,32,512]{2,1,0:T(8,128)(2,1)}), bf16[16,32,512]{2,1,0:T(8,128)(2,1)S(1)}, u32[]{:S(2)}, u32[]{:S(2)}) async-start(bf16[16,32,512]{2,1,0:T(8,128)(2,1)} %fusion.30), calls=%async_computation.14 | async-start | bytes 1048576 | tf_op jit(solution)/shard_map/all_to_all | solution.py:385
  299.6 8.5 %all-to-all-done.11 = bf16[16,32,512]{2,1,0:T(8,128)(2,1)S(1)} async-done(((bf16[16,32,512]{2,1,0:T(8,128)(2,1)}), bf16[16,32,512]{2,1,0:T(8,128)(2,1)S(1)}, u32[]{:S(2)}, u32[]{:S(2)}) %all-to-all-start.11) | async-done | bytes 524320 | tf_op jit(solution)/shard_map/all_to_all | solution.py:385
  308.1 3.7 %all-to-all-start.8 = ((bf16[16,128,256]{2,1,0:T(8,128)(2,1)}), bf16[16,128,256]{2,1,0:T(8,128)(2,1)S(1)}, u32[]{:S(2)}, u32[]{:S(2)}) async-start(bf16[16,128,256]{2,1,0:T(8,128)(2,1)} %bitcast.55), calls=%async_computation.9 | async-start | bytes 2097152 | tf_op jit(solution)/shard_map/all_to_all | solution.py:373
  314.8 12.5 %all-to-all-done.8 = bf16[16,128,256]{2,1,0:T(8,128)(2,1)S(1)} async-done(((bf16[16,128,256]{2,1,0:T(8,128)(2,1)}), bf16[16,128,256]{2,1,0:T(8,128)(2,1)S(1)}, u32[]{:S(2)}, u32[]{:S(2)}) %all-to-all-start.8) | async-done | bytes 1048608 | tf_op jit(solution)/shard_map/all_to_all | solution.py:373
  329.2 3.4 all-to-all-start.12
  332.7 5.5 %all-to-all-done.12 = bf16[4,128,256]{2,1,0:T(8,128)(2,1)S(1)} async-done(((bf16[4,128,256]{2,1,0:T(8,128)(2,1)}), bf16[4,128,256]{2,1,0:T(8,128)(2,1)S(1)}, u32[]{:S(2)}, u32[]{:S(2)}) %all-to-all-start.12) | async-done | bytes 262176 | tf_op jit(solution)/shard_map/all_to_all | solution.py:391
  338.2 4.2 %collective-permute-start.13 = (f32[2,64,256]{2,1,0:T(8,128)S(1)}, f32[2,64,256]{2,1,0:T(8,128)S(1)}, u32[]{:S(2)}, u32[]{:S(2)}) collective-permute-start(f32[2,64,256]{2,1,0:T(8,128)S(1)} %broadcast_select_fusion.4), channel_id=1, source_target_pairs={{0,4},{4,0},{1,5},{5,1},{2,6},{6,2},{3,7},{7,3},{8,12},{12,8},{9,1... | collective-permute-start | bytes 393224 | tf_op jit(solution)/shard_map/ppermute | solution.py:20
  (186 shorter events, 46.6 us)
Async XLA Ops:
  7.2 11.7 %copy-start = (bf16[1024,512]{1,0:T(8,128)(2,1)S(1)}, bf16[1024,512]{1,0:T(8,128)(2,1)}, u32[]{:S(2)}) copy-start(bf16[1024,512]{1,0:T(8,128)(2,1)} %param.16) | copy-start | bytes 3145732
  7.2 6.3 %copy-start.10 = (s32[1024]{0:T(1024)S(1)}, s32[1024]{0:T(1024)}, u32[]{:S(2)}) copy-start(s32[1024]{0:T(1024)} %param.14) | copy-start | bytes 12292
  7.2 6.3 %copy-start.9 = (s32[1024]{0:T(1024)S(1)}, s32[1024]{0:T(1024)}, u32[]{:S(2)}) copy-start(s32[1024]{0:T(1024)} %param.15) | copy-start | bytes 12292
  7.2 6.4 %copy-start.15 = (s32[1024]{0:T(1024)S(1)}, s32[1024]{0:T(1024)}, u32[]{:S(2)}) copy-start(s32[1024]{0:T(1024)} %param.11) | copy-start | bytes 12292
  7.2 6.4 %copy-start.16 = (s32[1024]{0:T(1024)S(1)}, s32[1024]{0:T(1024)}, u32[]{:S(2)}) copy-start(s32[1024]{0:T(1024)} %param.13) | copy-start | bytes 12292
  7.2 6.4 %copy-start.14 = (s32[1024]{0:T(1024)S(1)}, s32[1024]{0:T(1024)}, u32[]{:S(2)}) copy-start(s32[1024]{0:T(1024)} %param.12) | copy-start | bytes 12292
  7.2 67.0 %all-gather.6.cloned.1.call-start = ((), (), s32[]{:S(2)}) async-start(), calls=%async_computation.20 | async-start | bytes 2621440 | tf_op jit(solution)/shard_map/all_gather | solution.py:269
  9.6 37.0 %collective-permute-start.4 = (bf16[1024,256]{1,0:T(8,128)(2,1)}, bf16[1024,256]{1,0:T(8,128)(2,1)}, u32[]{:S(2)}, u32[]{:S(2)}) collective-permute-start(bf16[1024,256]{1,0:T(8,128)(2,1)} %get-tuple-element.45), channel_id=1, source_target_pairs={{0,3},{1,2},{2,1},{3,0},{4,7},{5,6},{6,5},{7,4},{8,11},{9,10},{10,... | collective-permute-start | bytes 1572872 | tf_op jit(solution)/shard_map/ppermute | solution.py:272
  12.9 33.7 %collective-permute-start.3 = (bf16[1024,256]{1,0:T(8,128)(2,1)}, bf16[1024,256]{1,0:T(8,128)(2,1)}, u32[]{:S(2)}, u32[]{:S(2)}) collective-permute-start(bf16[1024,256]{1,0:T(8,128)(2,1)} %get-tuple-element.45), channel_id=1, source_target_pairs={{0,2},{1,3},{2,0},{3,1},{4,6},{5,7},{6,4},{7,5},{8,10},{9,11},{10,... | collective-permute-start | bytes 1572872 | tf_op jit(solution)/shard_map/ppermute | solution.py:272
  13.4 33.2 %collective-permute-start.2 = (bf16[1024,256]{1,0:T(8,128)(2,1)}, bf16[1024,256]{1,0:T(8,128)(2,1)}, u32[]{:S(2)}, u32[]{:S(2)}) collective-permute-start(bf16[1024,256]{1,0:T(8,128)(2,1)} %get-tuple-element.45), channel_id=1, source_target_pairs={{0,1},{1,0},{2,3},{3,2},{4,5},{5,4},{6,7},{7,6},{8,9},{9,8},{10,11... | collective-permute-start | bytes 1572872 | tf_op jit(solution)/shard_map/ppermute | solution.py:272
  18.9 1.4 copy-start.7
  18.9 3.1 copy-start.12
  18.9 3.0 copy-start.13
  18.9 3.1 copy-start.11
  20.3 19.8 %copy-start.3 = (f32[1024,512]{1,0:T(8,128)}, f32[1024,512]{1,0:T(8,128)S(1)}, u32[]{:S(2)}) copy-start(f32[1024,512]{1,0:T(8,128)S(1)} %get-tuple-element.100) | copy-start | bytes 6291460
  20.3 2.5 collective-permute-start
  23.4 14.4 %all-to-all-start = ((f32[16,1,1024]{2,1,0:T(1,128)}), f32[16,1,1024]{2,1,0:T(1,128)S(1)}, u32[]{:S(2)}, u32[]{:S(2)}) async-start(f32[16,1,1024]{2,1,0:T(1,128)} %broadcast_in_dim.30), calls=%async_computation | async-start | bytes 131072 | tf_op jit(solution)/shard_map/all_to_all | solution.py:25
  40.0 29.2 %all-to-all-start.1 = ((bf16[4,304,512]{2,1,0:T(8,128)(2,1)}), bf16[4,304,512]{2,1,0:T(8,128)(2,1)S(1)}, u32[]{:S(2)}, u32[]{:S(2)}) async-start(bf16[4,304,512]{2,1,0:T(8,128)(2,1)} %pad_maximum_fusion.1), calls=%async_computation.1 | async-start | bytes 2490368 | tf_op jit(solution)/shard_map/all_to_all | solution.py:306
  44.1 77.6 %all-gather.4.cloned.1.call-start = ((), (), s32[]{:S(2)}) async-start(), calls=%async_computation.16 | async-start | bytes 5242880 | tf_op jit(solution)/shard_map/all_gather | solution.py:277
  70.4 3.8 %collective-permute-start.1 = (bf16[256,2048]{1,0:T(8,128)(2,1)}, bf16[256,2048]{1,0:T(8,128)(2,1)}, u32[]{:S(2)}, u32[]{:S(2)}) collective-permute-start(bf16[256,2048]{1,0:T(8,128)(2,1)} %pad_maximum_fusion.2.refs_0_), channel_id=1, source_target_pairs={{0,4},{4,0},{1,5},{5,1},{2,6},{6,2},{3,7},{7,3},{8,12},{12,8},{9,1... | collective-permute-start | bytes 3145736 | tf_op jit(solution)/shard_map/ppermute | solution.py:20
  82.1 14.6 %all-to-all-start.2 = ((f32[16,1,2048]{2,1,0:T(1,128)}), f32[16,1,2048]{2,1,0:T(1,128)S(1)}, u32[]{:S(2)}, u32[]{:S(2)}) async-start(f32[16,1,2048]{2,1,0:T(1,128)} %broadcast_in_dim.32), calls=%async_computation.2 | async-start | bytes 262144 | tf_op jit(solution)/shard_map/all_to_all | solution.py:25
  97.5 8.1 %all-to-all-start.3 = ((f32[4,1,2048]{2,1,0:T(1,128)}), f32[4,1,2048]{2,1,0:T(1,128)S(1)}, u32[]{:S(2)}, u32[]{:S(2)}) async-start(f32[4,1,2048]{2,1,0:T(1,128)} %broadcast_in_dim.33), calls=%async_computation.3 | async-start | bytes 65536 | tf_op jit(solution)/shard_map/all_to_all | solution.py:25
  108.3 5.3 %collective-permute-start.5 = (bf16[512,1024]{1,0:T(8,128)(2,1)S(1)}, bf16[512,1024]{1,0:T(8,128)(2,1)S(1)}, u32[]{:S(2)}, u32[]{:S(2)}) collective-permute-start(bf16[512,1024]{1,0:T(8,128)(2,1)S(1)} %pad_maximum_fusion.3), channel_id=1, source_target_pairs={{0,4},{4,0},{1,5},{5,1},{2,6},{6,2},{3,7},{7,3},{8,12},{12,8},{9,1... | collective-permute-start | bytes 3145736 | tf_op jit(solution)/shard_map/ppermute | solution.py:20
  113.9 7.7 %copy-start.8 = (bf16[512,2048]{1,0:T(8,128)(2,1)}, bf16[512,2048]{1,0:T(8,128)(2,1)S(1)}, u32[]{:S(2)}) copy-start(bf16[512,2048]{1,0:T(8,128)(2,1)S(1)} %slice_dynamic-update-slice_fusion.refs_0_) | copy-start | bytes 6291460
  128.2 23.3 %copy-start.5 = (f32[512,1024]{1,0:T(8,128)S(1)}, f32[512,1024]{1,0:T(8,128)}, u32[]{:S(2)}) copy-start(f32[512,1024]{1,0:T(8,128)} %get-tuple-element.19) | copy-start | bytes 6291460
  130.1 21.0 %all-to-all-start.4 = ((f32[64,1,2048]{2,1,0:T(1,128)}), f32[64,1,2048]{2,1,0:T(1,128)S(1)}, u32[]{:S(2)}, u32[]{:S(2)}) async-start(f32[64,1,2048]{2,1,0:T(1,128)} %broadcast_in_dim.34), calls=%async_computation.4 | async-start | bytes 1048576 | tf_op jit(solution)/shard_map/all_to_all | solution.py:25
  140.2 149.2 %reduce-scatter.6.cloned.1.call-start = ((), (), s32[]{:S(2)}) async-start(), calls=%async_computation.18 | async-start | bytes 5242880 | tf_op jit(solution)/shard_map/reduce_scatter | solution.py:349
  152.9 5.4 %collective-permute-start.6 = (f32[512,64]{0,1:T(8,128)S(1)}, f32[512,64]{0,1:T(8,128)S(1)}, u32[]{:S(2)}, u32[]{:S(2)}) collective-permute-start(f32[512,64]{0,1:T(8,128)S(1)} %pad_maximum_fusion.10), channel_id=1, source_target_pairs={{0,4},{4,0},{1,5},{5,1},{2,6},{6,2},{3,7},{7,3},{8,12},{12,8},{9,1... | collective-permute-start | bytes 393224 | tf_op jit(solution)/shard_map/ppermute | solution.py:20
  157.0 1.3 collective-permute-start.7
  189.5 107.7 %reduce-scatter.4.cloned.1.call-start = ((), (), s32[]{:S(2)}) async-start(), calls=%async_computation.17 | async-start | bytes 5242880 | tf_op jit(solution)/shard_map/reduce_scatter | solution.py:371
  195.9 5.1 %collective-permute-start.8 = (bf16[512,1024]{1,0:T(8,128)(2,1)}, bf16[512,1024]{1,0:T(8,128)(2,1)}, u32[]{:S(2)}, u32[]{:S(2)}) collective-permute-start(bf16[512,1024]{1,0:T(8,128)(2,1)} %get-tuple-element.21), channel_id=1, source_target_pairs={{0,4},{4,0},{1,5},{5,1},{2,6},{6,2},{3,7},{7,3},{8,12},{12,8},{9,1... | collective-permute-start | bytes 3145736 | tf_op jit(solution)/shard_map/ppermute | solution.py:20
  198.1 2.2 collective-permute-start.9
  200.3 1.6 copy-start.2
  236.7 90.7 %reduce-scatter.8.cloned.1.call-start = ((), (), s32[]{:S(2)}) async-start(), calls=%async_computation.19 | async-start | bytes 1310720 | tf_op jit(solution)/shard_map/reduce_scatter | solution.py:350
  243.4 5.4 %collective-permute-start.10 = (bf16[256,2048]{1,0:T(8,128)(2,1)}, bf16[256,2048]{1,0:T(8,128)(2,1)S(1)}, u32[]{:S(2)}, u32[]{:S(2)}) collective-permute-start(bf16[256,2048]{1,0:T(8,128)(2,1)} %get-tuple-element.23), channel_id=1, source_target_pairs={{0,4},{4,0},{1,5},{5,1},{2,6},{6,2},{3,7},{7,3},{8,12},{12,8},{9,1... | collective-permute-start | bytes 3145736 | tf_op jit(solution)/shard_map/ppermute | solution.py:20
  250.7 17.5 %copy-start.4 = (f32[1024,512]{1,0:T(8,128)S(1)}, f32[1024,512]{1,0:T(8,128)}, u32[]{:S(2)}) copy-start(f32[1024,512]{1,0:T(8,128)} %copy-done.3) | copy-start | bytes 6291460
  271.1 2.1 collective-permute-start.11
  286.2 1.4 copy-start.6
  287.6 3.4 collective-permute-start.12
  293.6 14.5 %all-to-all-start.11 = ((bf16[16,32,512]{2,1,0:T(8,128)(2,1)}), bf16[16,32,512]{2,1,0:T(8,128)(2,1)S(1)}, u32[]{:S(2)}, u32[]{:S(2)}) async-start(bf16[16,32,512]{2,1,0:T(8,128)(2,1)} %fusion.30), calls=%async_computation.14 | async-start | bytes 1048576 | tf_op jit(solution)/shard_map/all_to_all | solution.py:385
  308.1 19.1 %all-to-all-start.8 = ((bf16[16,128,256]{2,1,0:T(8,128)(2,1)}), bf16[16,128,256]{2,1,0:T(8,128)(2,1)S(1)}, u32[]{:S(2)}, u32[]{:S(2)}) async-start(bf16[16,128,256]{2,1,0:T(8,128)(2,1)} %bitcast.55), calls=%async_computation.9 | async-start | bytes 2097152 | tf_op jit(solution)/shard_map/all_to_all | solution.py:373
  312.5 20.2 %collective-permute-start.14 = (f32[4,256]{1,0:T(4,128)S(1)}, f32[4,256]{1,0:T(4,128)S(1)}, u32[]{:S(2)}, u32[]{:S(2)}) collective-permute-start(f32[4,256]{1,0:T(4,128)S(1)} %fusion.55), channel_id=1, source_target_pairs={{0,4},{4,0},{1,5},{5,1},{2,6},{6,2},{3,7},{7,3},{8,12},{12,8},{9,1... | collective-permute-start | bytes 12296 | tf_op jit(solution)/shard_map/ppermute | solution.py:20
  327.2 17.2 %copy-start.1 = (bf16[1024,512]{1,0:T(8,128)(2,1)S(1)}, bf16[1024,512]{1,0:T(8,128)(2,1)}, u32[]{:S(2)}) copy-start(bf16[1024,512]{1,0:T(8,128)(2,1)} %param.16) | copy-start | bytes 3145732
  329.2 8.9 %all-to-all-start.12 = ((bf16[4,128,256]{2,1,0:T(8,128)(2,1)}), bf16[4,128,256]{2,1,0:T(8,128)(2,1)S(1)}, u32[]{:S(2)}, u32[]{:S(2)}) async-start(bf16[4,128,256]{2,1,0:T(8,128)(2,1)} %bitcast.73), calls=%async_computation.15 | async-start | bytes 524288 | tf_op jit(solution)/shard_map/all_to_all | solution.py:391
  338.2 5.5 %collective-permute-start.13 = (f32[2,64,256]{2,1,0:T(8,128)S(1)}, f32[2,64,256]{2,1,0:T(8,128)S(1)}, u32[]{:S(2)}, u32[]{:S(2)}) collective-permute-start(f32[2,64,256]{2,1,0:T(8,128)S(1)} %broadcast_select_fusion.4), channel_id=1, source_target_pairs={{0,4},{4,0},{1,5},{5,1},{2,6},{6,2},{3,7},{7,3},{8,12},{12,8},{9,1... | collective-permute-start | bytes 393224 | tf_op jit(solution)/shard_map/ppermute | solution.py:20
Sparse Core Ops, SparseCore 0:
  13.6 49.6 all-gather.5
  65.0 56.5 all-gather.3
  189.7 44.0 reduce-scatter.5
  236.8 46.0 reduce-scatter.3
  289.6 17.9 reduce-scatter.7
where the time goes:
time: 353 us; the launch traced here: 351 us
  waiting for transfers between devices  95.4 us (27%)
  starting transfers between devices  70.6 us (20%)
  blocking collectives  63.5 us (18%)
  other arithmetic  43.7 us (12%)
  Pallas kernels  38.1 us (11%)
  local copies, waits for them, and re-layouts  16.2 us (5%)
  between operations  14.7 us (4%)
  matrix products  8.81 us (2%)
    all_to_all x4, starting transfers between devices, from_everyone(): lax.all_to_all(jnp.broadcast_to(array[None], (size, *array.shape)), axis,...  29 us
    all_to_all x4, waiting for transfers between devices, from_everyone(): lax.all_to_all(jnp.broadcast_to(array[None], (size, *array.shape)), axis,...  28.6 us
    all_to_all x2, blocking collectives, from_everyone(): lax.all_to_all(jnp.broadcast_to(array[None], (size, *array.shape)), axis,...  26.5 us
    ppermute x12, starting transfers between devices, swap_cores(): return lax.ppermute(array, 'c', [(0, 1), (1, 0)])  22.8 us
    all_to_all x1, waiting for transfers between devices, step(): message = lax.all_to_all(message, 'x', 0, 0, tiled=True)  20.8 us
    all_to_all x1, blocking collectives, step(): u1 = lax.all_to_all(u1_own, 'x', 1, 0, tiled=True).astype(float32)  17.4 us
    pallas_call x2, Pallas kernels, layer_dot(): pl.pallas_call(body, grid=(width // block,), in_specs=[pl.BlockSpec((part...  12.9 us
    all_to_all x1, waiting for transfers between devices, step(): lax.all_to_all(dw2.reshape(height * mp, -1, half), ('y', 'x'), 0, 0, tile...  12.5 us
  transfers between devices with their start and end apart: 28, of which 17 were waited for; matrix products, arithmetic and copies ran while one was open for 15% of the time, Pallas kernels for 7%

commit v1 on v0

--- a/solution.py
+++ b/solution.py
@@ -129,36 +129,32 @@
     )(*inputs, *weights)
 
 
-def back_dot(slopes, weights, half):
+def back_dot(slopes, weights, half, offset, dtype, flip):
     rows, width = slopes.shape
     middle = rows // 2
-
-    def body(slope_ref, weight_ref, keep_ref, send_ref):
-        product = dot_back(slope_ref[...], weight_ref[...])
-        keep_ref[...] = product[:, :half]
-        send_ref[:middle, :] = product[middle:, half:].astype(bfloat16)
-        send_ref[middle:, :] = product[:middle, half:].astype(bfloat16)
-
     units = weights.shape[0] // 2
+
+    def body(slope_ref, weight_ref, out_ref):
+        product = dot_back(slope_ref[...], weight_ref[...]).astype(dtype)
+        if flip:
+            out_ref[:middle, :] = product[middle:]
+            out_ref[middle:, :] = product[:middle]
+        else:
+            out_ref[...] = product
+
     return pl.pallas_call(
         body,
         grid=(units // half,),
         in_specs=[
             pl.BlockSpec(slopes.shape, lambda n: (0, 0)),
-            pl.BlockSpec((2 * half, width), lambda n: (n, 0)),
+            pl.BlockSpec((half, width), lambda n: (2 * n + offset, 0)),
         ],
-        out_specs=[
-            pl.BlockSpec((rows, half), lambda n: (0, n)),
-            pl.BlockSpec((rows, half), lambda n: (0, n)),
-        ],
-        out_shape=[
-            jax.ShapeDtypeStruct((rows, units), float32),
-            jax.ShapeDtypeStruct((rows, units), bfloat16),
-        ],
+        out_specs=pl.BlockSpec((rows, half), lambda n: (0, n)),
+        out_shape=jax.ShapeDtypeStruct((rows, units), dtype),
         cost_estimate=pl.CostEstimate(
-            flops=4 * rows * width * units,
+            flops=2 * rows * width * units,
             transcendentals=0,
-            bytes_accessed=2 * slopes.size + 2 * weights.size + 6 * rows * units,
+            bytes_accessed=2 * slopes.size + weights.size + 3 * rows * units,
         ),
     )(slopes, weights)
 
@@ -190,18 +186,16 @@
     )(*inputs, slopes)
 
 
-def split_back_dot(slopes, top, end):
+def split_back_dot(slopes, top, end, part_at, dtype):
     rows, width = slopes.shape
     middle = rows // 2
     units = top.shape[0]
     block = min(512, units)
     steps = units // block
 
-    def body(slope_ref, top_ref, end_ref, keep_ref, send_ref):
+    def body(slope_ref, top_ref, end_ref, out_ref):
         def write(weight_ref):
-            product = dot_back(slope_ref[...], weight_ref[...])
-            keep_ref[...] = product[:middle]
-            send_ref[...] = product[middle:].astype(bfloat16)
+            out_ref[...] = dot_back(slope_ref[...], weight_ref[...]).astype(dtype)
 
         at = pl.program_id(0)
         pl.when(at < steps)(lambda: write(top_ref))
@@ -211,22 +205,16 @@
         body,
         grid=(2 * steps,),
         in_specs=[
-            pl.BlockSpec(slopes.shape, lambda n: (0, 0)),
+            pl.BlockSpec((middle, width), lambda n: (part_at, 0)),
             pl.BlockSpec((block, width), lambda n: (jnp.minimum(n, steps - 1), 0)),
             pl.BlockSpec((block, width), lambda n: (jnp.maximum(n - steps, 0), 0)),
         ],
-        out_specs=[
-            pl.BlockSpec((middle, block), lambda n: (0, n)),
-            pl.BlockSpec((middle, block), lambda n: (0, n)),
-        ],
-        out_shape=[
-            jax.ShapeDtypeStruct((middle, 2 * units), float32),
-            jax.ShapeDtypeStruct((middle, 2 * units), bfloat16),
-        ],
+        out_specs=pl.BlockSpec((middle, block), lambda n: (0, n)),
+        out_shape=jax.ShapeDtypeStruct((middle, 2 * units), dtype),
         cost_estimate=pl.CostEstimate(
-            flops=4 * rows * width * units,
+            flops=4 * middle * width * units,
             transcendentals=0,
-            bytes_accessed=2 * slopes.size + 4 * units * width + 12 * middle * units,
+            bytes_accessed=slopes.size + 4 * units * width + 6 * middle * units,
         ),
     )(slopes, top, end)
 
@@ -343,8 +331,8 @@
     e3 = (gain3 * inv3 * (s3 - bias_sum3 / batch_total - n3 * gain_sum3 / batch_total)).astype(
         bfloat16
     )
-    u2_keep, u2_send = back_dot(e3, w3, half)
-    u2 = u2_keep + swap_cores(u2_send).astype(float32)
+    u2_far = swap_cores(back_dot(e3, w3, half, 1, bfloat16, True))
+    u2 = back_dot(e3, w3, half, 0, float32, False) + u2_far.astype(float32)
     dw3 = weight_dot((x2_all,), e3)
     dw3 = lax.psum_scatter(dw3, "z", scatter_dimension=0, tiled=True)
     dw3 = lax.psum_scatter(dw3, "x", scatter_dimension=1, tiled=True)
@@ -364,8 +352,9 @@
     e2 = (gain2 * inv2 * (s2 - bias_sum2 / batch_total - n2 * gain_sum2 / batch_total)).astype(
         bfloat16
     )
-    u1_keep, u1_send = split_back_dot(e2, w2_top, w2_end)
-    u1_own = (u1_keep + swap_cores(u1_send).astype(float32)).astype(bfloat16)
+    u1_far = swap_cores(split_back_dot(e2, w2_top, w2_end, 1, bfloat16))
+    u1_own = split_back_dot(e2, w2_top, w2_end, 0, float32) + u1_far.astype(float32)
+    u1_own = u1_own.astype(bfloat16)
     u1 = lax.all_to_all(u1_own, "x", 1, 0, tiled=True).astype(float32)
     dw2 = weight_dot((x1_own, x1_other), e2)
     dw2 = lax.psum_scatter(dw2, "z", scatter_dimension=0, tiled=True)

time: 353 us -> 357 us (1.011)
  Pallas kernels: 38.1 us -> 46 us
    pallas_call x1 -> x2, Pallas kernels: 6.62 us -> 10.8 us  [split_back_dot(): pl.pallas_call(body, grid=(2 * steps,), in_specs=[pl.BlockSpec((middle, w...]
    pallas_call x1 -> x2, Pallas kernels: 6.34 us -> 10.2 us  [back_dot(): pl.pallas_call(body, grid=(units // half,), in_specs=[pl.BlockSpec(slopes...]
  transfers between devices with their start and end apart: 28 -> 28, of which waited for: 17 -> 16; matrix products, arithmetic and copies ran while one was open for 15% -> 15% of each run, Pallas kernels for 7% -> 9%
where the time goes in v1:
time: 357 us; the launch traced here: 355 us
  waiting for transfers between devices  92.9 us (26%)
  starting transfers between devices  70.3 us (20%)
  blocking collectives  63.3 us (18%)
  Pallas kernels  46 us (13%)
  other arithmetic  43.8 us (12%)
  local copies, waits for them, and re-layouts  15.4 us (4%)
  between operations  14.7 us (4%)
  matrix products  8.77 us (2%)
    all_to_all x4, starting transfers between devices, from_everyone(): lax.all_to_all(jnp.broadcast_to(array[None], (size, *array.shape)), axis,...  29 us
    all_to_all x4, waiting for transfers between devices, from_everyone(): lax.all_to_all(jnp.broadcast_to(array[None], (size, *array.shape)), axis,...  28.6 us
    all_to_all x2, blocking collectives, from_everyone(): lax.all_to_all(jnp.broadcast_to(array[None], (size, *array.shape)), axis,...  26.4 us
    ppermute x12, starting transfers between devices, swap_cores(): return lax.ppermute(array, 'c', [(0, 1), (1, 0)])  22.7 us
    all_to_all x1, waiting for transfers between devices, step(): message = lax.all_to_all(message, 'x', 0, 0, tiled=True)  20.8 us
    all_to_all x1, blocking collectives, step(): u1 = lax.all_to_all(u1_own, 'x', 1, 0, tiled=True).astype(float32)  17.4 us
    pallas_call x2, Pallas kernels, layer_dot(): pl.pallas_call(body, grid=(width // block,), in_specs=[pl.BlockSpec((part...  12.9 us
    all_to_all x1, waiting for transfers between devices, step(): lax.all_to_all(dw2.reshape(height * mp, -1, half), ('y', 'x'), 0, 0, tile...  12.5 us
  transfers between devices with their start and end apart: 28, of which 16 were waited for; matrix products, arithmetic and copies ran while one was open for 15% of the time, Pallas kernels for 9%

profile of v1, /device:TPU:1, one launch (start us, length us, event | category | flops | bytes accessed | tf_op | source)
XLA Modules:
  0.0 355.2 jit_solution(2902409954780945586)
XLA Ops:
  7.3 2.3 dynamic-slice_bitcast_fusion
  9.6 3.3 collective-permute-start.4
  13.6 5.2 %fusion.5 = bf16[1024,1024]{1,0:T(8,128)(2,1)S(1)} fusion(f32[1024]{0:T(1024)S(1)} %get-tuple-element.88, f32[1024]{0:T(1024)S(1)} %convert_element_type.129, f32[1024]{0:T(1024)S(1)} %get-tuple-element.87, f32[1024]{0:T(1024)S(1)} %convert_element_type.128, f32[1024]{0:T(1024)S(1)} %get-tuple-element.86, f32[1024]{0:T(1024)S(1)} %convert_element_type.126, ...), kind=kLoop, calls=%fused_computation.9 | loop fusion | flops 37748736 | bytes 2134016 | tf_op jit(solution)/shard_map/convert_element_type | solution.py:62
  23.5 7.9 %all-to-all-start = ((f32[16,1,1024]{2,1,0:T(1,128)}), f32[16,1,1024]{2,1,0:T(1,128)S(1)}, u32[]{:S(2)}, u32[]{:S(2)}) async-start(f32[16,1,1024]{2,1,0:T(1,128)} %broadcast_in_dim.30), calls=%async_computation | async-start | bytes 131072 | tf_op jit(solution)/shard_map/all_to_all | solution.py:25
  31.4 6.5 %all-to-all-done = f32[16,1,1024]{2,1,0:T(1,128)S(1)} async-done(((f32[16,1,1024]{2,1,0:T(1,128)}), f32[16,1,1024]{2,1,0:T(1,128)S(1)}, u32[]{:S(2)}, u32[]{:S(2)}) %all-to-all-start) | async-done | bytes 65568 | tf_op jit(solution)/shard_map/all_to_all | solution.py:25
  40.1 4.0 %all-to-all-start.1 = ((bf16[4,304,512]{2,1,0:T(8,128)(2,1)}), bf16[4,304,512]{2,1,0:T(8,128)(2,1)S(1)}, u32[]{:S(2)}, u32[]{:S(2)}) async-start(bf16[4,304,512]{2,1,0:T(8,128)(2,1)} %pad_maximum_fusion.1), calls=%async_computation.1 | async-start | bytes 2490368 | tf_op jit(solution)/shard_map/all_to_all | solution.py:294
  48.4 20.8 %all-to-all-done.1 = bf16[4,304,512]{2,1,0:T(8,128)(2,1)S(1)} async-done(((bf16[4,304,512]{2,1,0:T(8,128)(2,1)}), bf16[4,304,512]{2,1,0:T(8,128)(2,1)S(1)}, u32[]{:S(2)}, u32[]{:S(2)}) %all-to-all-start.1) | async-done | bytes 1245216 | tf_op jit(solution)/shard_map/all_to_all | solution.py:294
  74.2 6.4 %shard_map.146 = (f32[512,1024]{1,0:T(8,128)}, f32[2,1024]{1,0:T(2,128)}) custom-call(bf16[256,2048]{1,0:T(8,128)(2,1)} %pad_maximum_fusion.2.refs_0_, bf16[256,2048]{1,0:T(8,128)(2,1)} %collective-permute-done.1.refs_1_, bf16[1024,1024]{1,0:T(8,128)(2,1)} %bitcast.139, bf16[1024,1024]{1,0:T(8,128)(2,1)} %pad_maximum_fusion.refs_3_.end_ref), custom_call_target="tpu_custom_call" | custom-call | flops 2147483648 | bytes 8388608 | tf_op jit(solution)/shard_map/pallas_call | solution.py:111
  82.1 7.8 %all-to-all-start.2 = ((f32[16,1,2048]{2,1,0:T(1,128)}), f32[16,1,2048]{2,1,0:T(1,128)S(1)}, u32[]{:S(2)}, u32[]{:S(2)}) async-start(f32[16,1,2048]{2,1,0:T(1,128)} %broadcast_in_dim.32), calls=%async_computation.2 | async-start | bytes 262144 | tf_op jit(solution)/shard_map/all_to_all | solution.py:25
  89.9 6.8 %all-to-all-done.2 = f32[16,1,2048]{2,1,0:T(1,128)S(1)} async-done(((f32[16,1,2048]{2,1,0:T(1,128)}), f32[16,1,2048]{2,1,0:T(1,128)S(1)}, u32[]{:S(2)}, u32[]{:S(2)}) %all-to-all-start.2) | async-done | bytes 131104 | tf_op jit(solution)/shard_map/all_to_all | solution.py:25
  97.5 3.3 all-to-all-start.3
  100.8 4.8 %all-to-all-done.3 = f32[4,1,2048]{2,1,0:T(1,128)S(1)} async-done(((f32[4,1,2048]{2,1,0:T(1,128)}), f32[4,1,2048]{2,1,0:T(1,128)S(1)}, u32[]{:S(2)}, u32[]{:S(2)}) %all-to-all-start.3) | async-done | bytes 32800 | tf_op jit(solution)/shard_map/all_to_all | solution.py:25
  105.6 2.5 fusion.9
  108.3 3.0 collective-permute-start.5
  111.4 2.2 collective-permute-done.5
  113.9 7.8 %all-gather.4.cloned.1.call-done.refs_1_.weight_ref = bf16[2048,1024]{1,0:T(8,128)(2,1)} async-done(((bf16[2048,256]{1,0:T(8,128)(2,1)}), bf16[2048,1024]{1,0:T(8,128)(2,1)}) %all-gather.4.cloned.1.call-update) | async-done | bytes 4194320 | tf_op jit(solution)/shard_map/all_gather | solution.py:265
  121.7 6.5 %shard_map.147 = (f32[512,1024]{1,0:T(8,128)}, f32[2,1024]{1,0:T(2,128)}) custom-call(bf16[512,2048]{1,0:T(8,128)(2,1)} %copy-done.8, bf16[2048,1024]{1,0:T(8,128)(2,1)} %all-gather.4.cloned.1.call-done.refs_1_.weight_ref), custom_call_target="tpu_custom_call" | custom-call | flops 2147483648 | bytes 8388608 | tf_op jit(solution)/shard_map/pallas_call | solution.py:111
  130.2 10.1 %all-to-all-start.4 = ((f32[64,1,2048]{2,1,0:T(1,128)}), f32[64,1,2048]{2,1,0:T(1,128)S(1)}, u32[]{:S(2)}, u32[]{:S(2)}) async-start(f32[64,1,2048]{2,1,0:T(1,128)} %broadcast_in_dim.34), calls=%async_computation.4 | async-start | bytes 1048576 | tf_op jit(solution)/shard_map/all_to_all | solution.py:25
  140.6 10.5 %all-to-all-done.4 = f32[64,1,2048]{2,1,0:T(1,128)S(1)} async-done(((f32[64,1,2048]{2,1,0:T(1,128)}), f32[64,1,2048]{2,1,0:T(1,128)S(1)}, u32[]{:S(2)}, u32[]{:S(2)}) %all-to-all-start.4) | async-done | bytes 524320 | tf_op jit(solution)/shard_map/all_to_all | solution.py:25
  152.9 3.3 collective-permute-start.6
  158.3 3.0 fusion.64
  161.6 17.3 %all_to_all.73 = f32[64,1,2048]{2,1,0:T(1,128)} all-to-all(f32[64,1,2048]{2,1,0:T(1,128)S(1)} %broadcast_in_dim.35), channel_id=1, replica_groups=mesh['z'=4,'y'=4,'c'=2,'x'=4] {'z','y','x'}, dimensions={0} | all-to-all | bytes 1048576 | tf_op jit(solution)/shard_map/all_to_all | solution.py:25
  180.3 3.2 multiply_convert_fusion.2.slope_ref.refs_1_
  183.5 6.0 %shard_map.151 = bf16[2048,1024]{1,0:T(8,128)(2,1)} custom-call(bf16[512,2048]{1,0:T(8,128)(2,1)} %copy-done.8, bf16[512,1024]{1,0:T(8,128)(2,1)} %multiply_convert_fusion.2.slope_ref.refs_1_), custom_call_target="tpu_custom_call" | custom-call | flops 2147483648 | bytes 7340032 | tf_op jit(solution)/shard_map/pallas_call | solution.py:174
  189.6 4.9 %shard_map.149 = bf16[512,1024]{1,0:T(8,128)(2,1)} custom-call(bf16[512,1024]{1,0:T(8,128)(2,1)} %multiply_convert_fusion.2.slope_ref.refs_1_, bf16[2048,1024]{1,0:T(8,128)(2,1)} %all-gather.4.cloned.1.call-done.refs_1_.weight_ref), custom_call_target="tpu_custom_call" | custom-call | flops 1073741824 | bytes 4718592 | tf_op jit(solution)/shard_map/pallas_call | solution.py:145
  196.7 2.1 collective-permute-done.9
  199.5 5.2 %shard_map.148 = f32[512,1024]{1,0:T(8,128)} custom-call(bf16[512,1024]{1,0:T(8,128)(2,1)} %multiply_convert_fusion.2.slope_ref.refs_1_, bf16[2048,1024]{1,0:T(8,128)(2,1)} %all-gather.4.cloned.1.call-done.refs_1_.weight_ref), custom_call_target="tpu_custom_call" | custom-call | flops 1073741824 | bytes 4718592 | tf_op jit(solution)/shard_map/pallas_call | solution.py:145
  204.7 4.8 %fusion.63 = (f32[1024]{0:T(1024)S(1)}, f32[1024]{0:T(1024)S(1)}, f32[512,1024]{1,0:T(8,128)}) fusion(f32[1024]{0:T(1024)S(1)} %bitcast.166, f32[512,1024]{1,0:T(8,128)S(1)} %copy-done.2, f32[1024]{0:T(1024)S(1)} %bitcast.169, f32[1024]{0:T(1024)S(1)} %bitcast.172, f32[1024]{0:T(1024)S(1)} %bitcast.164, f32[512,1024]{1,0:T(8,128)} %shard_map.148, ...), kind=kLoop, calls=%fused_computation.203 | loop fusion | flops 11532288 | bytes 7364608 | tf_op jit(solution)/shard_map/reduce_sum | solution.py:341
  210.0 12.1 %all_to_all.74 = f32[16,1,6144]{2,1,0:T(1,128)S(1)} all-to-all(f32[16,1,6144]{2,1,0:T(1,128)S(1)} %copy.75), channel_id=1, replica_groups=mesh['z'=4,'y'=4,'c'=2,'x'=4] {'y','x'}, dimensions={0} | all-to-all | bytes 786432 | tf_op jit(solution)/shard_map/all_to_all | solution.py:345
  222.5 7.4 %all_to_all.75 = f32[4,1,3072]{2,1,0:T(1,128)S(1)} all-to-all(f32[4,1,3072]{2,1,0:T(1,128)S(1)} %broadcast_in_dim.38), channel_id=1, replica_groups=mesh['z'=4,'y'=4,'c'=2,'x'=4] {'z'}, dimensions={0} | all-to-all | bytes 98304 | tf_op jit(solution)/shard_map/all_to_all | solution.py:349
  230.0 3.3 multiply_convert_fusion.1.refs_2_.slope_ref
  233.2 6.2 %shard_map.150 = bf16[2048,1024]{1,0:T(8,128)(2,1)} custom-call(bf16[256,2048]{1,0:T(8,128)(2,1)} %pad_maximum_fusion.2.refs_0_, bf16[256,2048]{1,0:T(8,128)(2,1)} %collective-permute-done.1.refs_1_, bf16[512,1024]{1,0:T(8,128)(2,1)} %multiply_convert_fusion.1.refs_2_.slope_ref), custom_call_target="tpu_custom_call" | custom-call | flops 2147483648 | bytes 7340032 | tf_op jit(solution)/shard_map/pallas_call | solution.py:174
  239.5 5.3 %shard_map.153 = bf16[256,2048]{1,0:T(8,128)(2,1)} custom-call(bf16[512,1024]{1,0:T(8,128)(2,1)} %multiply_convert_fusion.1.refs_2_.slope_ref, bf16[1024,1024]{1,0:T(8,128)(2,1)} %bitcast.140, bf16[1024,1024]{1,0:T(8,128)(2,1)} %pad_maximum_fusion.refs_3_.end_ref), custom_call_target="tpu_custom_call" | custom-call | flops 1073741824 | bytes 6291456 | tf_op jit(solution)/shard_map/pallas_call | solution.py:204
  244.8 2.8 collective-permute-start.10
  247.6 5.5 %shard_map.152 = f32[256,2048]{1,0:T(8,128)} custom-call(bf16[512,1024]{1,0:T(8,128)(2,1)} %multiply_convert_fusion.1.refs_2_.slope_ref, bf16[1024,1024]{1,0:T(8,128)(2,1)} %bitcast.141, bf16[1024,1024]{1,0:T(8,128)(2,1)} %pad_maximum_fusion.refs_3_.end_ref), custom_call_target="tpu_custom_call" | custom-call | flops 1073741824 | bytes 6291456 | tf_op jit(solution)/shard_map/pallas_call | solution.py:204
  253.1 1.9 add_convert_fusion
  255.1 17.4 %all_to_all.76 = bf16[256,4,512]{2,0,1:T(8,128)(2,1)S(1)} all-to-all(bf16[256,4,512]{2,0,1:T(8,128)(2,1)S(1)} %bitcast.147), channel_id=1, replica_groups=mesh['z'=4,'y'=4,'c'=2,'x'=4] {'x'}, dimensions={1} | all-to-all | bytes 2097152 | tf_op jit(solution)/shard_map/all_to_all | solution.py:358
  272.4 2.9 fusion.62
  277.6 9.2 %all_to_all.77 = f32[16,1,1024]{2,1,0:T(1,128)S(1)} all-to-all(f32[16,1,1024]{2,1,0:T(1,128)S(1)} %broadcast_in_dim.41), channel_id=1, replica_groups=mesh['z'=4,'y'=4,'c'=2,'x'=4] {'z','y'}, dimensions={0} | all-to-all | bytes 131072 | tf_op jit(solution)/shard_map/all_to_all | solution.py:25
  286.8 3.6 %fusion.27 = f32[1024,512]{1,0:T(8,128)S(1)} fusion(bf16[1024,1024]{1,0:T(8,128)(2,1)} %copy-done.7, f32[1024,512]{1,0:T(8,128)} %get-tuple-element.29, f32[1024,512]{1,0:T(8,128)S(1)} %copy-done.4, f32[512]{0:T(512)S(1)} %bitcast.217, f32[512]{0:T(512)S(1)} %bitcast.219, f32[512]{0:T(512)S(1)} %bitcast.218, f32[512]{0:T(512)S(1)} %bitcast.190, ...), kind=kOutput, calls=%fused_computation.63 | convolution fusion | flops 1077936128 | bytes 8398848 | tf_op jit(solution)/shard_map/dot_general | solution.py:83
  295.3 2.6 fusion.30
  297.9 3.6 %all-to-all-start.11 = ((bf16[16,32,512]{2,1,0:T(8,128)(2,1)}), bf16[16,32,512]{2,1,0:T(8,128)(2,1)S(1)}, u32[]{:S(2)}, u32[]{:S(2)}) async-start(bf16[16,32,512]{2,1,0:T(8,128)(2,1)} %fusion.30), calls=%async_computation.14 | async-start | bytes 1048576 | tf_op jit(solution)/shard_map/all_to_all | solution.py:374
  304.0 8.5 %all-to-all-done.11 = bf16[16,32,512]{2,1,0:T(8,128)(2,1)S(1)} async-done(((bf16[16,32,512]{2,1,0:T(8,128)(2,1)}), bf16[16,32,512]{2,1,0:T(8,128)(2,1)S(1)}, u32[]{:S(2)}, u32[]{:S(2)}) %all-to-all-start.11) | async-done | bytes 524320 | tf_op jit(solution)/shard_map/all_to_all | solution.py:374
  312.4 3.7 %all-to-all-start.8 = ((bf16[16,128,256]{2,1,0:T(8,128)(2,1)}), bf16[16,128,256]{2,1,0:T(8,128)(2,1)S(1)}, u32[]{:S(2)}, u32[]{:S(2)}) async-start(bf16[16,128,256]{2,1,0:T(8,128)(2,1)} %bitcast.55), calls=%async_computation.9 | async-start | bytes 2097152 | tf_op jit(solution)/shard_map/all_to_all | solution.py:362
  319.1 12.5 %all-to-all-done.8 = bf16[16,128,256]{2,1,0:T(8,128)(2,1)S(1)} async-done(((bf16[16,128,256]{2,1,0:T(8,128)(2,1)}), bf16[16,128,256]{2,1,0:T(8,128)(2,1)S(1)}, u32[]{:S(2)}, u32[]{:S(2)}) %all-to-all-start.8) | async-done | bytes 1048608 | tf_op jit(solution)/shard_map/all_to_all | solution.py:362
  333.5 3.4 all-to-all-start.12
  337.0 5.5 %all-to-all-done.12 = bf16[4,128,256]{2,1,0:T(8,128)(2,1)S(1)} async-done(((bf16[4,128,256]{2,1,0:T(8,128)(2,1)}), bf16[4,128,256]{2,1,0:T(8,128)(2,1)S(1)}, u32[]{:S(2)}, u32[]{:S(2)}) %all-to-all-start.12) | async-done | bytes 262176 | tf_op jit(solution)/shard_map/all_to_all | solution.py:380
  342.5 4.2 %collective-permute-start.13 = (f32[2,64,256]{2,1,0:T(8,128)S(1)}, f32[2,64,256]{2,1,0:T(8,128)S(1)}, u32[]{:S(2)}, u32[]{:S(2)}) collective-permute-start(f32[2,64,256]{2,1,0:T(8,128)S(1)} %broadcast_select_fusion.4), channel_id=1, source_target_pairs={{0,4},{4,0},{1,5},{5,1},{2,6},{6,2},{3,7},{7,3},{8,12},{12,8},{9,1... | collective-permute-start | bytes 393224 | tf_op jit(solution)/shard_map/ppermute | solution.py:20
  (188 shorter events, 47.6 us)
Async XLA Ops:
  7.2 11.7 %copy-start = (bf16[1024,512]{1,0:T(8,128)(2,1)S(1)}, bf16[1024,512]{1,0:T(8,128)(2,1)}, u32[]{:S(2)}) copy-start(bf16[1024,512]{1,0:T(8,128)(2,1)} %param.16) | copy-start | bytes 3145732
  7.2 6.3 %copy-start.10 = (s32[1024]{0:T(1024)S(1)}, s32[1024]{0:T(1024)}, u32[]{:S(2)}) copy-start(s32[1024]{0:T(1024)} %param.14) | copy-start | bytes 12292
  7.2 6.3 %copy-start.9 = (s32[1024]{0:T(1024)S(1)}, s32[1024]{0:T(1024)}, u32[]{:S(2)}) copy-start(s32[1024]{0:T(1024)} %param.15) | copy-start | bytes 12292
  7.2 6.4 %copy-start.15 = (s32[1024]{0:T(1024)S(1)}, s32[1024]{0:T(1024)}, u32[]{:S(2)}) copy-start(s32[1024]{0:T(1024)} %param.11) | copy-start | bytes 12292
  7.2 6.4 %copy-start.16 = (s32[1024]{0:T(1024)S(1)}, s32[1024]{0:T(1024)}, u32[]{:S(2)}) copy-start(s32[1024]{0:T(1024)} %param.13) | copy-start | bytes 12292
  7.2 6.4 %copy-start.14 = (s32[1024]{0:T(1024)S(1)}, s32[1024]{0:T(1024)}, u32[]{:S(2)}) copy-start(s32[1024]{0:T(1024)} %param.12) | copy-start | bytes 12292
  7.2 67.0 %all-gather.6.cloned.1.call-start = ((), (), s32[]{:S(2)}) async-start(), calls=%async_computation.20 | async-start | bytes 2621440 | tf_op jit(solution)/shard_map/all_gather | solution.py:257
  9.6 37.0 %collective-permute-start.4 = (bf16[1024,256]{1,0:T(8,128)(2,1)}, bf16[1024,256]{1,0:T(8,128)(2,1)}, u32[]{:S(2)}, u32[]{:S(2)}) collective-permute-start(bf16[1024,256]{1,0:T(8,128)(2,1)} %get-tuple-element.37), channel_id=1, source_target_pairs={{0,3},{1,2},{2,1},{3,0},{4,7},{5,6},{6,5},{7,4},{8,11},{9,10},{10,... | collective-permute-start | bytes 1572872 | tf_op jit(solution)/shard_map/ppermute | solution.py:260
  12.9 33.7 %collective-permute-start.3 = (bf16[1024,256]{1,0:T(8,128)(2,1)}, bf16[1024,256]{1,0:T(8,128)(2,1)}, u32[]{:S(2)}, u32[]{:S(2)}) collective-permute-start(bf16[1024,256]{1,0:T(8,128)(2,1)} %get-tuple-element.37), channel_id=1, source_target_pairs={{0,2},{1,3},{2,0},{3,1},{4,6},{5,7},{6,4},{7,5},{8,10},{9,11},{10,... | collective-permute-start | bytes 1572872 | tf_op jit(solution)/shard_map/ppermute | solution.py:260
  13.4 33.2 %collective-permute-start.2 = (bf16[1024,256]{1,0:T(8,128)(2,1)}, bf16[1024,256]{1,0:T(8,128)(2,1)}, u32[]{:S(2)}, u32[]{:S(2)}) collective-permute-start(bf16[1024,256]{1,0:T(8,128)(2,1)} %get-tuple-element.37), channel_id=1, source_target_pairs={{0,1},{1,0},{2,3},{3,2},{4,5},{5,4},{6,7},{7,6},{8,9},{9,8},{10,11... | collective-permute-start | bytes 1572872 | tf_op jit(solution)/shard_map/ppermute | solution.py:260
  18.9 1.4 copy-start.7
  18.9 3.1 copy-start.12
  18.9 3.1 copy-start.13
  18.9 3.1 copy-start.11
  20.3 19.8 %copy-start.3 = (f32[1024,512]{1,0:T(8,128)}, f32[1024,512]{1,0:T(8,128)S(1)}, u32[]{:S(2)}) copy-start(f32[1024,512]{1,0:T(8,128)S(1)} %get-tuple-element.92) | copy-start | bytes 6291460
  20.3 2.5 collective-permute-start
  23.5 14.4 %all-to-all-start = ((f32[16,1,1024]{2,1,0:T(1,128)}), f32[16,1,1024]{2,1,0:T(1,128)S(1)}, u32[]{:S(2)}, u32[]{:S(2)}) async-start(f32[16,1,1024]{2,1,0:T(1,128)} %broadcast_in_dim.30), calls=%async_computation | async-start | bytes 131072 | tf_op jit(solution)/shard_map/all_to_all | solution.py:25
  40.1 29.2 %all-to-all-start.1 = ((bf16[4,304,512]{2,1,0:T(8,128)(2,1)}), bf16[4,304,512]{2,1,0:T(8,128)(2,1)S(1)}, u32[]{:S(2)}, u32[]{:S(2)}) async-start(bf16[4,304,512]{2,1,0:T(8,128)(2,1)} %pad_maximum_fusion.1), calls=%async_computation.1 | async-start | bytes 2490368 | tf_op jit(solution)/shard_map/all_to_all | solution.py:294
  44.1 77.6 %all-gather.4.cloned.1.call-start = ((), (), s32[]{:S(2)}) async-start(), calls=%async_computation.16 | async-start | bytes 5242880 | tf_op jit(solution)/shard_map/all_gather | solution.py:265
  70.4 3.8 %collective-permute-start.1 = (bf16[256,2048]{1,0:T(8,128)(2,1)}, bf16[256,2048]{1,0:T(8,128)(2,1)}, u32[]{:S(2)}, u32[]{:S(2)}) collective-permute-start(bf16[256,2048]{1,0:T(8,128)(2,1)} %pad_maximum_fusion.2.refs_0_), channel_id=1, source_target_pairs={{0,4},{4,0},{1,5},{5,1},{2,6},{6,2},{3,7},{7,3},{8,12},{12,8},{9,1... | collective-permute-start | bytes 3145736 | tf_op jit(solution)/shard_map/ppermute | solution.py:20
  82.1 14.6 %all-to-all-start.2 = ((f32[16,1,2048]{2,1,0:T(1,128)}), f32[16,1,2048]{2,1,0:T(1,128)S(1)}, u32[]{:S(2)}, u32[]{:S(2)}) async-start(f32[16,1,2048]{2,1,0:T(1,128)} %broadcast_in_dim.32), calls=%async_computation.2 | async-start | bytes 262144 | tf_op jit(solution)/shard_map/all_to_all | solution.py:25
  97.5 8.1 %all-to-all-start.3 = ((f32[4,1,2048]{2,1,0:T(1,128)}), f32[4,1,2048]{2,1,0:T(1,128)S(1)}, u32[]{:S(2)}, u32[]{:S(2)}) async-start(f32[4,1,2048]{2,1,0:T(1,128)} %broadcast_in_dim.33), calls=%async_computation.3 | async-start | bytes 65536 | tf_op jit(solution)/shard_map/all_to_all | solution.py:25
  108.3 5.3 %collective-permute-start.5 = (bf16[512,1024]{1,0:T(8,128)(2,1)S(1)}, bf16[512,1024]{1,0:T(8,128)(2,1)S(1)}, u32[]{:S(2)}, u32[]{:S(2)}) collective-permute-start(bf16[512,1024]{1,0:T(8,128)(2,1)S(1)} %pad_maximum_fusion.3), channel_id=1, source_target_pairs={{0,4},{4,0},{1,5},{5,1},{2,6},{6,2},{3,7},{7,3},{8,12},{12,8},{9,1... | collective-permute-start | bytes 3145736 | tf_op jit(solution)/shard_map/ppermute | solution.py:20
  113.9 7.8 %copy-start.8 = (bf16[512,2048]{1,0:T(8,128)(2,1)}, bf16[512,2048]{1,0:T(8,128)(2,1)S(1)}, u32[]{:S(2)}) copy-start(bf16[512,2048]{1,0:T(8,128)(2,1)S(1)} %slice_dynamic-update-slice_fusion.refs_0_) | copy-start | bytes 6291460
  128.2 23.3 %copy-start.5 = (f32[512,1024]{1,0:T(8,128)S(1)}, f32[512,1024]{1,0:T(8,128)}, u32[]{:S(2)}) copy-start(f32[512,1024]{1,0:T(8,128)} %get-tuple-element.15) | copy-start | bytes 6291460
  130.2 21.0 %all-to-all-start.4 = ((f32[64,1,2048]{2,1,0:T(1,128)}), f32[64,1,2048]{2,1,0:T(1,128)S(1)}, u32[]{:S(2)}, u32[]{:S(2)}) async-start(f32[64,1,2048]{2,1,0:T(1,128)} %broadcast_in_dim.34), calls=%async_computation.4 | async-start | bytes 1048576 | tf_op jit(solution)/shard_map/all_to_all | solution.py:25
  140.2 153.5 %reduce-scatter.6.cloned.1.call-start = ((), (), s32[]{:S(2)}) async-start(), calls=%async_computation.18 | async-start | bytes 5242880 | tf_op jit(solution)/shard_map/reduce_scatter | solution.py:337
  152.9 5.4 %collective-permute-start.6 = (f32[512,64]{0,1:T(8,128)S(1)}, f32[512,64]{0,1:T(8,128)S(1)}, u32[]{:S(2)}, u32[]{:S(2)}) collective-permute-start(f32[512,64]{0,1:T(8,128)S(1)} %pad_maximum_fusion.10), channel_id=1, source_target_pairs={{0,4},{4,0},{1,5},{5,1},{2,6},{6,2},{3,7},{7,3},{8,12},{12,8},{9,1... | collective-permute-start | bytes 393224 | tf_op jit(solution)/shard_map/ppermute | solution.py:20
  157.1 1.3 collective-permute-start.7
  189.6 112.0 %reduce-scatter.4.cloned.1.call-start = ((), (), s32[]{:S(2)}) async-start(), calls=%async_computation.17 | async-start | bytes 5242880 | tf_op jit(solution)/shard_map/reduce_scatter | solution.py:360
  194.5 10.2 %collective-permute-start.8 = (bf16[512,1024]{1,0:T(8,128)(2,1)}, bf16[512,1024]{1,0:T(8,128)(2,1)}, u32[]{:S(2)}, u32[]{:S(2)}) collective-permute-start(bf16[512,1024]{1,0:T(8,128)(2,1)} %shard_map.149), channel_id=1, source_target_pairs={{0,4},{4,0},{1,5},{5,1},{2,6},{6,2},{3,7},{7,3},{8,12},{12,8},{9,1... | collective-permute-start | bytes 3145736 | tf_op jit(solution)/shard_map/ppermute | solution.py:20
  196.6 2.2 collective-permute-start.9
  199.5 5.2 %copy-start.2 = (f32[512,1024]{1,0:T(8,128)S(1)}, f32[512,1024]{1,0:T(8,128)}, u32[]{:S(2)}) copy-start(f32[512,1024]{1,0:T(8,128)} %get-tuple-element.13) | copy-start | bytes 6291460
  239.4 92.3 %reduce-scatter.8.cloned.1.call-start = ((), (), s32[]{:S(2)}) async-start(), calls=%async_computation.19 | async-start | bytes 1310720 | tf_op jit(solution)/shard_map/reduce_scatter | solution.py:338
  244.8 8.3 %collective-permute-start.10 = (bf16[256,2048]{1,0:T(8,128)(2,1)}, bf16[256,2048]{1,0:T(8,128)(2,1)S(1)}, u32[]{:S(2)}, u32[]{:S(2)}) collective-permute-start(bf16[256,2048]{1,0:T(8,128)(2,1)} %shard_map.153), channel_id=1, source_target_pairs={{0,4},{4,0},{1,5},{5,1},{2,6},{6,2},{3,7},{7,3},{8,12},{12,8},{9,1... | collective-permute-start | bytes 3145736 | tf_op jit(solution)/shard_map/ppermute | solution.py:20
  255.0 17.5 %copy-start.4 = (f32[1024,512]{1,0:T(8,128)S(1)}, f32[1024,512]{1,0:T(8,128)}, u32[]{:S(2)}) copy-start(f32[1024,512]{1,0:T(8,128)} %copy-done.3) | copy-start | bytes 6291460
  275.4 2.1 collective-permute-start.11
  290.4 1.4 copy-start.6
  291.9 3.4 collective-permute-start.12
  297.9 14.5 %all-to-all-start.11 = ((bf16[16,32,512]{2,1,0:T(8,128)(2,1)}), bf16[16,32,512]{2,1,0:T(8,128)(2,1)S(1)}, u32[]{:S(2)}, u32[]{:S(2)}) async-start(bf16[16,32,512]{2,1,0:T(8,128)(2,1)} %fusion.30), calls=%async_computation.14 | async-start | bytes 1048576 | tf_op jit(solution)/shard_map/all_to_all | solution.py:374
  312.4 19.1 %all-to-all-start.8 = ((bf16[16,128,256]{2,1,0:T(8,128)(2,1)}), bf16[16,128,256]{2,1,0:T(8,128)(2,1)S(1)}, u32[]{:S(2)}, u32[]{:S(2)}) async-start(bf16[16,128,256]{2,1,0:T(8,128)(2,1)} %bitcast.55), calls=%async_computation.9 | async-start | bytes 2097152 | tf_op jit(solution)/shard_map/all_to_all | solution.py:362
  316.8 20.2 %collective-permute-start.14 = (f32[4,256]{1,0:T(4,128)S(1)}, f32[4,256]{1,0:T(4,128)S(1)}, u32[]{:S(2)}, u32[]{:S(2)}) collective-permute-start(f32[4,256]{1,0:T(4,128)S(1)} %fusion.55), channel_id=1, source_target_pairs={{0,4},{4,0},{1,5},{5,1},{2,6},{6,2},{3,7},{7,3},{8,12},{12,8},{9,1... | collective-permute-start | bytes 12296 | tf_op jit(solution)/shard_map/ppermute | solution.py:20
  331.5 17.2 %copy-start.1 = (bf16[1024,512]{1,0:T(8,128)(2,1)S(1)}, bf16[1024,512]{1,0:T(8,128)(2,1)}, u32[]{:S(2)}) copy-start(bf16[1024,512]{1,0:T(8,128)(2,1)} %param.16) | copy-start | bytes 3145732
  333.5 8.9 %all-to-all-start.12 = ((bf16[4,128,256]{2,1,0:T(8,128)(2,1)}), bf16[4,128,256]{2,1,0:T(8,128)(2,1)S(1)}, u32[]{:S(2)}, u32[]{:S(2)}) async-start(bf16[4,128,256]{2,1,0:T(8,128)(2,1)} %bitcast.73), calls=%async_computation.15 | async-start | bytes 524288 | tf_op jit(solution)/shard_map/all_to_all | solution.py:380
  342.5 5.5 %collective-permute-start.13 = (f32[2,64,256]{2,1,0:T(8,128)S(1)}, f32[2,64,256]{2,1,0:T(8,128)S(1)}, u32[]{:S(2)}, u32[]{:S(2)}) collective-permute-start(f32[2,64,256]{2,1,0:T(8,128)S(1)} %broadcast_select_fusion.4), channel_id=1, source_target_pairs={{0,4},{4,0},{1,5},{5,1},{2,6},{6,2},{3,7},{7,3},{8,12},{12,8},{9,1... | collective-permute-start | bytes 393224 | tf_op jit(solution)/shard_map/ppermute | solution.py:20
Sparse Core Ops, SparseCore 0:
  13.6 49.6 all-gather.5
  65.0 56.6 all-gather.3
  189.7 44.0 reduce-scatter.5
  239.5 44.6 reduce-scatter.3
  293.9 17.5 reduce-scatter.7
